TPU v7x, 256 devices: a whole 4x4x8 slice. The times are simulated.
256 devices in a mesh: grp: 16 (over z_lo, y, core), seq: 16 (over z_hi, x).
Axes of the slice: x: 4, y: 4, z: 8 (z_hi: 4, z_lo: 2; z = z_hi * 2 + z_lo), core: 2. Of those that a mesh axis runs over, the one named last changes fastest.
Arguments:
- query: bfloat16 [16, 4096, 640], P('grp', 'seq'), may hold values from -64 to 64
- resp_kv: bfloat16 [16, 4096, 256], P('grp', 'seq'), may hold values from -6 to 6
- prompt_kv: bfloat16 [16, 4096, 256], P('grp', 'seq'), may hold values from -64 to 64
- grad_out: bfloat16 [16, 4096, 640], P('grp', 'seq'), may hold values from -6 to 6
- rewards: float32 [16, 16], P('grp'), may hold values from -4 to 4
- lengths: int32 [16, 16], P('grp'), may hold values from 1 to 256, as said below
- block_order: int32 [16, 32], P('grp'), may hold values from 0 to 31, each once within a row
Outputs:
- grad_query: bfloat16 [16, 4096, 640], P('grp', 'seq')
- grad_stream: bfloat16 [16, 4096, 256], P('grp', 'seq')
- grad_prompt: bfloat16 [16, 4096, 256], P('grp', 'seq')
Inputs may be any that keep to these rules, and one draw needn't show every extreme that they name: `lengths`: each response has 1 to 256 tokens; some response has exactly 256. Each row of block_order names every response block of its group once.
All inputs are finite; a program needn't handle non-finite values.
Results may differ from a plain program's by a relative error of at most 0.015.
Values may be sent and summed in bfloat16 or wider, within the bound.
A program may use at most 128 MiB of HBM per device.

v0:
```python
from functools import partial
import jax
import jax.numpy as jnp
from jax import lax
from jax.sharding import Mesh
from jax.sharding import PartitionSpec as P

RESP = 16
BLK = 128
NB = 2
SEQ = ("seq_0", "seq_1")
LOSS_SCALE = 32.0
BIG_NEGATIVE = -1e30


def in_one_piece(arrays, axis, dim, along):
    widths = [a.shape[along] for a in arrays]
    both = jnp.concatenate(arrays, axis=along)
    filled = lax.all_gather(both, axis, axis=dim, tiled=True)
    return tuple(jnp.split(filled, [sum(widths[:k]) for k in range(1, len(widths))], axis=along))


def reduced_to_own(blocks, axes, sequence):
    inside = blocks.shape[1:]
    blocks = blocks.reshape(*(lax.axis_size(a) for a in axes), *inside)
    blocks = jnp.moveaxis(blocks, sequence, range(len(axes))).reshape(-1, *inside)
    for k in sequence:
        blocks = lax.psum_scatter(blocks, axes[k], scatter_dimension=0, tiled=True)
    return blocks[0]


def split_up(value, dim, size):
    dims = value.shape
    blocks = value.reshape(*dims[:dim], size, dims[dim] // size, *dims[dim + 1 :])
    return jnp.moveaxis(blocks, dim, 0)


def sum_by_axis(value, axes, sequence, dim):
    size = lax.axis_size(axes)
    return reduced_to_own(split_up(value, dim, size), axes, sequence)


def product(pattern, first_operand, second_operand):
    return jnp.einsum(pattern, first_operand, second_operand, preferred_element_type=jnp.float32)


def block_terms(query_block, weighted, prompt_pairs, own_pairs, positions):
    half_width = prompt_pairs.shape[1] // 2
    score_scale = half_width ** (-0.5)
    prompt_keys = prompt_pairs[:, :half_width]
    prompt_values = prompt_pairs[:, half_width:]
    own_keys = own_pairs[:, :half_width]
    own_values = own_pairs[:, half_width:]
    visible = (jnp.arange(own_pairs.shape[0], dtype=jnp.int32)[None, :] <= positions[:, None])[None]
    scores_prompt = product("thd,kd->htk", query_block, prompt_keys) * score_scale
    scores_own = jnp.where(
        visible, product("thd,kd->htk", query_block, own_keys) * score_scale, BIG_NEGATIVE
    )
    peak_score = jnp.maximum(jnp.max(scores_prompt, axis=2), jnp.max(scores_own, axis=2))
    expo_prompt = jnp.exp(scores_prompt - peak_score[..., None])
    expo_own = jnp.where(visible, jnp.exp(scores_own - peak_score[..., None]), 0.0)
    prob_total = jnp.sum(expo_prompt, axis=2) + jnp.sum(expo_own, axis=2)
    probs_prompt = expo_prompt / prob_total[..., None]
    probs_own = expo_own / prob_total[..., None]
    low_prompt = probs_prompt.astype(jnp.bfloat16)
    low_own = probs_own.astype(jnp.bfloat16)
    attended = product("htk,kd->thd", low_prompt, prompt_values) + product(
        "htk,kd->thd", low_own, own_values
    )
    row_delta = jnp.einsum("thd,thd->ht", weighted.astype(jnp.float32), attended)
    grad_prompt_scores = (
        probs_prompt * (product("thd,kd->htk", weighted, prompt_values) - row_delta[..., None])
    ).astype(jnp.bfloat16)
    grad_own_scores = (
        probs_own * (product("thd,kd->htk", weighted, own_values) - row_delta[..., None])
    ).astype(jnp.bfloat16)
    grad_query = (
        product("htk,kd->thd", grad_prompt_scores, prompt_keys)
        + product("htk,kd->thd", grad_own_scores, own_keys)
    ) * score_scale
    prompt_term = jnp.concatenate(
        [
            product("htk,thd->kd", grad_prompt_scores, query_block) * score_scale,
            product("htk,thd->kd", low_prompt, weighted),
        ],
        axis=1,
    )
    own_term = jnp.concatenate(
        [
            product("htk,thd->kd", grad_own_scores, query_block) * score_scale,
            product("htk,thd->kd", low_own, weighted),
        ],
        axis=1,
    )
    return (grad_query, prompt_term, own_term, peak_score, prob_total, row_delta)


def local(query, resp_kv, prompt_kv, grad_out, rewards, lengths, block_order):
    head_width = resp_kv.shape[2] // 2
    head_count = query.shape[2] // head_width
    row_count = query.shape[1]
    local_blocks = row_count // BLK
    capacity = NB * BLK
    group_count = lax.axis_size("grp")
    seq_count = lax.axis_size(SEQ)
    count = lax.psum(jnp.sum(lengths[0]).astype(jnp.float32), "grp")
    advantage = rewards[0] - jnp.mean(rewards[0])
    factor = advantage * (LOSS_SCALE * group_count * RESP * capacity) / count
    block_plan = block_order[0]
    inverse = jnp.argsort(block_plan)
    prompt_all, stream_all = in_one_piece((prompt_kv[0], resp_kv[0]), SEQ, 0, 1)
    blocks = stream_all.reshape(block_plan.shape[0], BLK, 2 * head_width)
    stored = lax.axis_index(SEQ) * local_blocks + jnp.arange(local_blocks, dtype=jnp.int32)
    stream_block = block_plan[stored]
    response = stream_block // NB
    positions = (stream_block % NB)[:, None] * BLK + jnp.arange(BLK, dtype=jnp.int32)[None, :]
    token_weight = jnp.where(
        positions < lengths[0][response][:, None], factor[response][:, None], 0.0
    )
    weighted = (
        grad_out[0].reshape(local_blocks, BLK, head_count * head_width).astype(jnp.float32)
        * token_weight[..., None]
    ).astype(jnp.bfloat16)
    weighted = weighted.reshape(local_blocks, BLK, head_count, head_width)
    queries = query[0].reshape(local_blocks, BLK, head_count, head_width)
    slot_table = inverse.reshape(RESP, NB)[response]
    block_items = (queries, weighted, slot_table, positions)

    def block_step(with_prompt, carried, block_item):
        prompt_sum, stream_sum = carried
        query_block, weight_block, slot_index, block_positions = block_item
        own_pairs = jnp.take(blocks, slot_index, axis=0).reshape(capacity, 2 * head_width)
        grad_query, prompt_term, own_term, peak_score, prob_total, row_delta = block_terms(
            query_block, weight_block, prompt_all, own_pairs, block_positions
        )
        stream_sum = stream_sum.at[slot_index].add(own_term.reshape(NB, BLK, 2 * head_width))
        prompt_sum = prompt_sum + prompt_term
        return (
            (prompt_sum, stream_sum),
            (grad_query.astype(jnp.bfloat16), peak_score, prob_total, row_delta),
        )

    stream_zero = jnp.zeros((block_plan.shape[0], BLK, 2 * head_width), jnp.float32)
    initial = (jnp.zeros((prompt_all.shape[0], 2 * head_width), jnp.float32), stream_zero)
    (prompt_sum, stream_sum), block_outputs = lax.scan(
        partial(block_step, True), initial, block_items
    )
    prompt_grad = sum_by_axis(prompt_sum.astype(jnp.bfloat16), SEQ, (1, 0), 0).astype(jnp.float32)
    grad_rows = block_outputs[0]
    outgoing = stream_sum.reshape(seq_count, local_blocks * BLK, 2 * head_width)
    incoming = lax.all_to_all(
        outgoing.astype(jnp.bfloat16), SEQ, split_axis=0, concat_axis=0, tiled=True
    ).astype(outgoing.dtype)
    stream_grad = jnp.sum(incoming, axis=0)
    grad_query = grad_rows.reshape(row_count, head_count * head_width)
    return (
        grad_query[None],
        stream_grad.astype(jnp.bfloat16)[None],
        prompt_grad.astype(jnp.bfloat16)[None],
    )


def solution(mesh):
    split = Mesh(mesh.devices.reshape(mesh.shape["grp"], 4, 4), ("grp", "seq_0", "seq_1"))
    placed = (
        P("grp", SEQ, None),
        P("grp", SEQ, None),
        P("grp", SEQ, None),
        P("grp", SEQ, None),
        P("grp", None),
        P("grp", None),
        P("grp", None),
    )
    return jax.shard_map(
        local,
        mesh=split,
        in_specs=placed,
        out_specs=(P("grp", SEQ, None), P("grp", SEQ, None), P("grp", SEQ, None)),
        check_vma=False,
    )
```

profile of v0, /device:TPU:2, one launch (start us, length us, event | category | flops | bytes accessed | tf_op | source)
XLA Modules:
  0.0 268.5 jit_solution(16111596052325326619)
XLA Ops:
  7.2 1.7 pad_maximum_fusion.1
  10.9 32.3 %psum.7 = f32[]{:T(128)} all-reduce(f32[]{:T(128)S(6)} %convert_element_type.45), channel_id=1, replica_groups=mesh['grp'=16,'seq_0'=4,'seq_1'=4] {'grp'}, use_global_device_ids=true, to_apply=%region_2.0 | all-reduce | flops 1 | bytes 8 | tf_op jit(solution)/shard_map/psum | solution.py:106
  43.2 2.3 sort.17
  57.3 31.1 %all-gather.2.cloned.1.call-done = bf16[4096,512]{1,0:T(8,128)(2,1)} async-done(((bf16[256,512]{1,0:T(8,128)(2,1)}), bf16[4096,512]{1,0:T(8,128)(2,1)}) %all-gather.2.cloned.1.call-update) | async-done | bytes 4194320 | tf_op jit(solution)/shard_map/all_gather | solution.py:19
  88.4 3.8 %fusion.75 = (bf16[4096,256]{1,0:T(8,128)(2,1)}, bf16[4096,256]{1,0:T(8,128)(2,1)S(1)}) fusion(bf16[4096,512]{1,0:T(8,128)(2,1)} %all-gather.2.cloned.1.call-done), kind=kLoop, calls=%fused_computation.118 | loop fusion | bytes 8388608 | tf_op jit(solution)/shard_map/split | solution.py:20
  92.1 2.5 broadcast_in_dim.81
  94.6 73.7 %while.15 = (s32[]{:T(128)}, f32[4096,256]{0,1:T(8,128)}, f32[32,128,256]{2,1,0:T(8,128)}, bf16[2,128,5,128]{3,1,2,0:T(8,128)(2,1)}, bf16[2,128,5,128]{3,1,2,0:T...) while((s32[]{:T(128)}, f32[4096,256]{0,1:T(8,128)}, ...), condition=%wide.region_10.11_spmd.clone, body=%wide.region_4.10_spmd.clone.sunk | while | flops 4335778816 | bytes 192303536 | solution.py:145
  94.8 2.8 %gather_fusion = bf16[2,128,256]{2,1,0:T(8,128)(2,1)S(1)} fusion(bf16[32,128,256]{2,1,0:T(8,128)(2,1)} %get-tuple-element.235, s32[1024]{0:T(1024)S(1)} %pad_clamp_fusion.4), kind=kCustom, calls=%fused_computation.clone.clone.1 | custom fusion | bytes 262152 | tf_op jit(solution)/shard_map/while/body/eval_jaxpr/jit(_take)/gather | solution.py:132
  97.9 1.6 bitcast_reduce_fusion.2
  99.7 1.8 fusion.129
  103.5 2.2 fusion.131
  108.8 5.6 %convolution_bitcast_fusion.11 = f32[4096,128]{0,1:T(8,128)S(1)} fusion(bf16[2,128,5,128]{3,1,2,0:T(8,128)(2,1)} %get-tuple-element.236, s32[]{:T(128)S(6)} %copy.69, f32[128,5,4096]{2,0,1:T(8,128)} %copy-done, f32[5,128]{1,0:T(8,128)S(1)} %add.189, f32[5,128]{1,0:T(8,128)S(1)} %max.9), kind=kOutput, calls=%fused_computation.14.clone.1 | convolution fusion | flops 681574400 | bytes 12751876 | tf_op jit(solution)/shard_map/while/body/eval_jaxpr/htk,thd->kd/dot_general | solution.py:44
  115.8 4.4 %fusion.133 = bf16[5,128,4096]{2,1,0:T(8,128)(2,1)S(1)} fusion(f32[5,128]{1,0:T(8,128)S(1)} %fusion.132, bf16[4096,256]{1,0:T(8,128)(2,1)} %copy-done.1, bf16[2,128,5,128]{3,1,2,0:T(8,128)(2,1)} %get-tuple-element.236, s32[]{:T(128)S(6)} %copy.69, f32[5,128]{1,0:T(8,128)S(1)} %add.189, f32[5,128]{1,0:T(8,128)S(1)} %max.9, ...), kind=kOutput, calls=%fused_computation.8.clone.1 | convolution fusion | flops 686817280 | bytes 16948740 | tf_op jit(solution)/shard_map/while/body/eval_jaxpr/thd,kd->htk/dot_general | solution.py:44
  120.2 2.7 %convolution_bitcast_fusion.13 = f32[128,5,128]{2,0,1:T(8,128)S(1)} fusion(bf16[5,128,4096]{2,1,0:T(8,128)(2,1)S(1)} %fusion.133, bf16[4096,256]{1,0:T(8,128)(2,1)} %copy-done.1), kind=kOutput, calls=%fused_computation.36.clone.1 | convolution fusion | flops 671088640 | bytes 6619136 | tf_op jit(solution)/shard_map/while/body/eval_jaxpr/htk,kd->thd/dot_general | solution.py:44
  125.1 2.9 %maximum_add_fusion.2 = f32[4096,256]{0,1:T(8,128)} fusion(f32[4096,128]{0,1:T(8,128)S(1)} %convolution_bitcast_fusion.11, f32[4096,128]{0,1:T(8,128)S(1)} %fusion.134, f32[4096,256]{0,1:T(8,128)} %get-tuple-element.216, pred[]{:T(512)S(6)} %compare.21), kind=kLoop, calls=%fused_computation.17.clone.1 | loop fusion | flops 3145728 | bytes 12582913 | tf_op jit(solution)/shard_map/while/body/eval_jaxpr/add | solution.py:137
  128.0 2.3 scatter_fusion
  130.4 2.8 %gather_fusion = bf16[2,128,256]{2,1,0:T(8,128)(2,1)S(1)} fusion(bf16[32,128,256]{2,1,0:T(8,128)(2,1)} %get-tuple-element.235, s32[1024]{0:T(1024)S(1)} %pad_clamp_fusion.4), kind=kCustom, calls=%fused_computation.clone.clone.1 | custom fusion | bytes 262152 | tf_op jit(solution)/shard_map/while/body/eval_jaxpr/jit(_take)/gather | solution.py:132
  135.3 1.8 fusion.129
  139.2 2.2 fusion.131
  144.5 5.6 %convolution_bitcast_fusion.11 = f32[4096,128]{0,1:T(8,128)S(1)} fusion(bf16[2,128,5,128]{3,1,2,0:T(8,128)(2,1)} %get-tuple-element.236, s32[]{:T(128)S(6)} %copy.69, f32[128,5,4096]{2,0,1:T(8,128)} %copy-done, f32[5,128]{1,0:T(8,128)S(1)} %add.189, f32[5,128]{1,0:T(8,128)S(1)} %max.9), kind=kOutput, calls=%fused_computation.14.clone.1 | convolution fusion | flops 681574400 | bytes 12751876 | tf_op jit(solution)/shard_map/while/body/eval_jaxpr/htk,thd->kd/dot_general | solution.py:44
  151.5 4.4 %fusion.133 = bf16[5,128,4096]{2,1,0:T(8,128)(2,1)S(1)} fusion(f32[5,128]{1,0:T(8,128)S(1)} %fusion.132, bf16[4096,256]{1,0:T(8,128)(2,1)} %copy-done.1, bf16[2,128,5,128]{3,1,2,0:T(8,128)(2,1)} %get-tuple-element.236, s32[]{:T(128)S(6)} %copy.69, f32[5,128]{1,0:T(8,128)S(1)} %add.189, f32[5,128]{1,0:T(8,128)S(1)} %max.9, ...), kind=kOutput, calls=%fused_computation.8.clone.1 | convolution fusion | flops 686817280 | bytes 16948740 | tf_op jit(solution)/shard_map/while/body/eval_jaxpr/thd,kd->htk/dot_general | solution.py:44
  155.9 2.7 %convolution_bitcast_fusion.13 = f32[128,5,128]{2,0,1:T(8,128)S(1)} fusion(bf16[5,128,4096]{2,1,0:T(8,128)(2,1)S(1)} %fusion.133, bf16[4096,256]{1,0:T(8,128)(2,1)} %copy-done.1), kind=kOutput, calls=%fused_computation.36.clone.1 | convolution fusion | flops 671088640 | bytes 6619136 | tf_op jit(solution)/shard_map/while/body/eval_jaxpr/htk,kd->thd/dot_general | solution.py:44
  160.8 5.2 %maximum_add_fusion.2 = f32[4096,256]{0,1:T(8,128)} fusion(f32[4096,128]{0,1:T(8,128)S(1)} %convolution_bitcast_fusion.11, f32[4096,128]{0,1:T(8,128)S(1)} %fusion.134, f32[4096,256]{0,1:T(8,128)} %get-tuple-element.216, pred[]{:T(512)S(6)} %compare.21), kind=kLoop, calls=%fused_computation.17.clone.1 | loop fusion | flops 3145728 | bytes 12582913 | tf_op jit(solution)/shard_map/while/body/eval_jaxpr/add | solution.py:137
  166.0 2.3 scatter_fusion
  168.3 2.5 convert_element_type.49
  170.7 2.8 %reshape_reshape.3 = bf16[4,4,256,256]{2,1,0,3:T(4,128)(2,1)} reshape(bf16[4096,256]{0,1:T(8,128)(2,1)S(1)} %convert_element_type.49) | data formatting | bytes 4194304 | tf_op jit(solution)/shard_map/reshape;reshape | solution.py:25
  173.5 4.3 %copy.37 = bf16[4,4,256,256]{3,2,0,1:T(8,128)(2,1)} copy(bf16[4,4,256,256]{2,1,0,3:T(4,128)(2,1)} %reshape_reshape.3) | data formatting | bytes 4194304 | tf_op jit(solution)/shard_map/reshape;reshape | solution.py:25
  177.9 3.8 %convert_element_type.47 = bf16[32,128,256]{2,1,0:T(8,128)(2,1)} convert(f32[32,128,256]{2,1,0:T(8,128)} %get-tuple-element.60) | non-fusion elementwise | flops 1048576 | bytes 6291456 | tf_op jit(solution)/shard_map/convert_element_type | solution.py:152
  181.7 9.1 %all-to-all-start = ((bf16[16,256,256]{2,1,0:T(8,128)(2,1)}), bf16[16,256,256]{2,1,0:T(8,128)(2,1)S(1)}, u32[]{:S(2)}, u32[]{:S(2)}) async-start(bf16[16,256,256]{2,1,0:T(8,128)(2,1)} %bitcast.11), calls=%async_computation | async-start | bytes 4194304 | tf_op jit(solution)/shard_map/all_to_all | solution.py:151
  190.9 37.1 %reduce-scatter.3.cloned.1.call-done = bf16[4,256,256]{2,1,0:T(8,128)(2,1)} async-done(((bf16[16,256,256]{2,1,0:T(8,128)(2,1)}), bf16[4,256,256]{2,1,0:T(8,128)(2,1)}) %reduce-scatter.3.cloned.1.call-update) | async-done | bytes 524304 | tf_op jit(solution)/shard_map/reduce_scatter | solution.py:28
  229.4 10.1 %all-to-all-done = bf16[16,256,256]{2,1,0:T(8,128)(2,1)S(1)} async-done(((bf16[16,256,256]{2,1,0:T(8,128)(2,1)}), bf16[16,256,256]{2,1,0:T(8,128)(2,1)S(1)}, u32[]{:S(2)}, u32[]{:S(2)}) %all-to-all-start) | async-done | bytes 2097184 | tf_op jit(solution)/shard_map/all_to_all | solution.py:151
  240.4 21.5 %reduce-scatter.5.cloned.1.call-done = bf16[1,256,256]{2,1,0:T(8,128)(2,1)} async-done(((bf16[4,256,256]{2,1,0:T(8,128)(2,1)}), bf16[1,256,256]{2,1,0:T(8,128)(2,1)}) %reduce-scatter.5.cloned.1.call-update) | async-done | bytes 131088 | tf_op jit(solution)/shard_map/reduce_scatter | solution.py:28
  (108 shorter events, 34.8 us)
Async XLA Ops:
  7.2 81.2 %all-gather.2.cloned.1.call-start = ((), (), s32[]{:S(2)}) async-start(), calls=%async_computation.3 | async-start | bytes 4456448 | tf_op jit(solution)/shard_map/all_gather | solution.py:19
  8.9 219.1 %reduce-scatter.3.cloned.1.call-start = ((), (), s32[]{:S(2)}) async-start(), calls=%async_computation.4 | async-start | bytes 2621440 | tf_op jit(solution)/shard_map/reduce_scatter | solution.py:28
  94.6 11.1 %copy-start.1 = (bf16[4096,256]{1,0:T(8,128)(2,1)}, bf16[4096,256]{1,0:T(8,128)(2,1)S(1)}, u32[]{:S(2)}) copy-start(bf16[4096,256]{1,0:T(8,128)(2,1)S(1)} %get-tuple-element.232) | copy-start | bytes 6291460 | tf_op jit(solution)/shard_map/while
  99.5 4.0 %copy-start = (f32[128,5,4096]{2,0,1:T(8,128)}, f32[128,5,4096]{2,0,1:T(8,128)S(1)}, u32[]{:S(2)}) copy-start(f32[128,5,4096]{2,0,1:T(8,128)S(1)} %get-tuple-element.199) | copy-start | bytes 31457284 | tf_op jit(solution)/shard_map/while
  108.6 5.8 %slice-start = ((s8[10485760]{0:T(1024)(128)(4,1)}), s8[2097152]{0:T(1024)(128)(4,1)S(1)}, s32[]{:S(2)}) async-start(s8[10485760]{0:T(1024)(128)(4,1)} %bitcast.268), calls=%async_computation.6 | async-start | bytes 4194304 | tf_op jit(solution)/shard_map/while
  108.8 5.8 %slice-start.1 = ((s8[10485760]{0:T(1024)(128)(4,1)}), s8[4194304]{0:T(1024)(128)(4,1)S(1)}, s32[]{:S(2)}) async-start(s8[10485760]{0:T(1024)(128)(4,1)} %bitcast.268), calls=%async_computation.7 | async-start | bytes 8388608 | tf_op jit(solution)/shard_map/while
  108.8 7.0 %slice-start.2 = ((s8[10485760]{0:T(1024)(128)(4,1)}), s8[4194304]{0:T(1024)(128)(4,1)S(1)}, s32[]{:S(2)}) async-start(s8[10485760]{0:T(1024)(128)(4,1)} %bitcast.268), calls=%async_computation.8 | async-start | bytes 8388608 | tf_op jit(solution)/shard_map/while
  122.9 1.1 copy-start.3
  124.4 0.7 copy-start.4
  125.1 5.2 %copy-start.2 = (bf16[4096,256]{1,0:T(8,128)(2,1)S(1)}, bf16[4096,256]{1,0:T(8,128)(2,1)}, u32[]{:S(2)}) copy-start(bf16[4096,256]{1,0:T(8,128)(2,1)} %copy-done.1) | copy-start | bytes 6291460 | tf_op jit(solution)/shard_map/while
  130.3 11.1 %copy-start.1 = (bf16[4096,256]{1,0:T(8,128)(2,1)}, bf16[4096,256]{1,0:T(8,128)(2,1)S(1)}, u32[]{:S(2)}) copy-start(bf16[4096,256]{1,0:T(8,128)(2,1)S(1)} %get-tuple-element.232) | copy-start | bytes 6291460 | tf_op jit(solution)/shard_map/while
  135.2 4.0 %copy-start = (f32[128,5,4096]{2,0,1:T(8,128)}, f32[128,5,4096]{2,0,1:T(8,128)S(1)}, u32[]{:S(2)}) copy-start(f32[128,5,4096]{2,0,1:T(8,128)S(1)} %get-tuple-element.199) | copy-start | bytes 31457284 | tf_op jit(solution)/shard_map/while
  144.3 5.8 %slice-start = ((s8[10485760]{0:T(1024)(128)(4,1)}), s8[2097152]{0:T(1024)(128)(4,1)S(1)}, s32[]{:S(2)}) async-start(s8[10485760]{0:T(1024)(128)(4,1)} %bitcast.268), calls=%async_computation.6 | async-start | bytes 4194304 | tf_op jit(solution)/shard_map/while
  144.5 5.8 %slice-start.1 = ((s8[10485760]{0:T(1024)(128)(4,1)}), s8[4194304]{0:T(1024)(128)(4,1)S(1)}, s32[]{:S(2)}) async-start(s8[10485760]{0:T(1024)(128)(4,1)} %bitcast.268), calls=%async_computation.7 | async-start | bytes 8388608 | tf_op jit(solution)/shard_map/while
  144.5 7.0 %slice-start.2 = ((s8[10485760]{0:T(1024)(128)(4,1)}), s8[4194304]{0:T(1024)(128)(4,1)S(1)}, s32[]{:S(2)}) async-start(s8[10485760]{0:T(1024)(128)(4,1)} %bitcast.268), calls=%async_computation.8 | async-start | bytes 8388608 | tf_op jit(solution)/shard_map/while
  158.6 1.1 copy-start.3
  160.0 0.7 copy-start.4
  160.8 7.5 %copy-start.2 = (bf16[4096,256]{1,0:T(8,128)(2,1)S(1)}, bf16[4096,256]{1,0:T(8,128)(2,1)}, u32[]{:S(2)}) copy-start(bf16[4096,256]{1,0:T(8,128)(2,1)} %copy-done.1) | copy-start | bytes 6291460 | tf_op jit(solution)/shard_map/while
  177.9 50.2 %copy-start.5 = (bf16[2,128,5,128]{3,1,2,0:T(8,128)(2,1)S(1)}, bf16[2,128,5,128]{3,1,2,0:T(8,128)(2,1)}, u32[]{:S(2)}) copy-start(bf16[2,128,5,128]{3,1,2,0:T(8,128)(2,1)} %get-tuple-element.59) | copy-start | bytes 983044
  181.7 57.8 %all-to-all-start = ((bf16[16,256,256]{2,1,0:T(8,128)(2,1)}), bf16[16,256,256]{2,1,0:T(8,128)(2,1)S(1)}, u32[]{:S(2)}, u32[]{:S(2)}) async-start(bf16[16,256,256]{2,1,0:T(8,128)(2,1)} %bitcast.11), calls=%async_computation | async-start | bytes 4194304 | tf_op jit(solution)/shard_map/all_to_all | solution.py:151
  190.8 71.1 %reduce-scatter.5.cloned.1.call-start = ((), (), s32[]{:S(2)}) async-start(), calls=%async_computation.5 | async-start | bytes 655360 | tf_op jit(solution)/shard_map/reduce_scatter | solution.py:28
Sparse Core Ops, SparseCore 0:
  10.4 77.9 all-gather.1
  178.0 49.9 reduce-scatter.2
  231.1 30.7 reduce-scatter.4
where the time goes:
time: 269 us; the launch traced here: 268 us
  waiting for transfers between devices  99.8 us (37%)
  matrix products  45 us (17%)
  local copies, waits for them, and re-layouts  34.1 us (13%)
  other arithmetic  32.4 us (12%)
  blocking collectives  32.3 us (12%)
  between operations  15.1 us (6%)
  starting transfers between devices  9.26 us (3%)
    reduce_scatter x2, waiting for transfers between devices, reduced_to_own(): blocks = lax.psum_scatter(blocks, axes[k], scatter_dimension=0, tiled=True)  58.6 us
    dot_general x24, matrix products, product(): jnp.einsum(pattern, first_operand, second_operand, preferred_element_type...  45 us
    psum x1, blocking collectives, local(): count = lax.psum(jnp.sum(lengths[0]).astype(jnp.float32), 'grp')  32.3 us
    all_gather x1, waiting for transfers between devices, in_one_piece(): filled = lax.all_gather(both, axis, axis=dim, tiled=True)  31.1 us
    all_to_all x1, waiting for transfers between devices, local(): lax.all_to_all(outgoing.astype(jnp.bfloat16), SEQ, split_axis=0, concat_a...  10.1 us
    all_to_all x1, starting transfers between devices, local(): lax.all_to_all(outgoing.astype(jnp.bfloat16), SEQ, split_axis=0, concat_a...  9.15 us
    add x2, other arithmetic, block_step(): prompt_sum = prompt_sum + prompt_term  8.07 us
    another operation x2, local copies, waits for them, and re-layouts, reduced_to_own(): blocks = blocks.reshape(*(lax.axis_size(a) for a in axes), *inside)  7.1 us
  transfers between devices with their start and end apart: 4, of which 4 were waited for; matrix products, arithmetic and copies ran while one was open for 8% of the time, Pallas kernels for 0%

commit v1 on v0

--- a/solution.py
+++ b/solution.py
@@ -103,7 +103,7 @@
     capacity = NB * BLK
     group_count = lax.axis_size("grp")
     seq_count = lax.axis_size(SEQ)
-    count = lax.psum(jnp.sum(lengths[0]).astype(jnp.float32), "grp")
+    count = jnp.sum(lax.all_gather(jnp.sum(lengths[0]).astype(jnp.float32), "grp"), axis=0)
     advantage = rewards[0] - jnp.mean(rewards[0])
     factor = advantage * (LOSS_SCALE * group_count * RESP * capacity) / count
     block_plan = block_order[0]

time: 269 us -> 270 us (level)
    unnamed x0 -> x1, blocking collectives: none -> 32.3 us
    psum x1 -> x0, blocking collectives: 32.3 us -> none  [local(): count = lax.psum(jnp.sum(lengths[0]).astype(jnp.float32), 'grp')]
  transfers between devices with their start and end apart: 4 -> 4, of which waited for: 4 -> 4; matrix products, arithmetic and copies ran while one was open for 8% -> 9% of each run, Pallas kernels for 0% -> 0%
where the time goes in v1:
time: 270 us; the launch traced here: 269 us
  waiting for transfers between devices  97.9 us (36%)
  matrix products  45.1 us (17%)
  local copies, waits for them, and re-layouts  36.1 us (13%)
  other arithmetic  33.2 us (12%)
  blocking collectives  32.3 us (12%)
  between operations  15.1 us (6%)
  starting transfers between devices  9.25 us (3%)
    reduce_scatter x2, waiting for transfers between devices, reduced_to_own(): blocks = lax.psum_scatter(blocks, axes[k], scatter_dimension=0, tiled=True)  60.2 us
    dot_general x24, matrix products, product(): jnp.einsum(pattern, first_operand, second_operand, preferred_element_type...  45.1 us
    unnamed x1, blocking collectives  32.3 us
    all_gather x1, waiting for transfers between devices, in_one_piece(): filled = lax.all_gather(both, axis, axis=dim, tiled=True)  29.2 us
    all_to_all x1, starting transfers between devices, local(): lax.all_to_all(outgoing.astype(jnp.bfloat16), SEQ, split_axis=0, concat_a...  9.13 us
    all_to_all x1, waiting for transfers between devices, local(): lax.all_to_all(outgoing.astype(jnp.bfloat16), SEQ, split_axis=0, concat_a...  8.42 us
    add x2, other arithmetic, block_step(): prompt_sum = prompt_sum + prompt_term  8.07 us
    another operation x2, local copies, waits for them, and re-layouts, reduced_to_own(): blocks = blocks.reshape(*(lax.axis_size(a) for a in axes), *inside)  7.1 us
  transfers between devices with their start and end apart: 4, of which 4 were waited for; matrix products, arithmetic and copies ran while one was open for 9% of the time, Pallas kernels for 0%

profile of v1, /device:TPU:2, one launch (start us, length us, event | category | flops | bytes accessed | tf_op | source)
XLA Modules:
  0.0 269.4 jit_solution(12663245096783217022)
XLA Ops:
  7.2 1.7 pad_maximum_fusion.1
  14.2 32.3 %all-reduce = f32[16]{0:T(128)S(1)} all-reduce(f32[16]{0:T(128)S(1)} %dynamic-update-slice), channel_id=1, replica_groups=mesh['grp'=16,'seq_0'=4,'seq_1'=4] {'grp'}, use_global_device_ids=true, to_apply=%add | all-reduce | flops 16 | bytes 128
  47.3 2.3 sort.17
  60.1 29.2 %all-gather.2.cloned.1.call-done = bf16[4096,512]{1,0:T(8,128)(2,1)} async-done(((bf16[256,512]{1,0:T(8,128)(2,1)}), bf16[4096,512]{1,0:T(8,128)(2,1)}) %all-gather.2.cloned.1.call-update) | async-done | bytes 4194320 | tf_op jit(solution)/shard_map/all_gather | solution.py:19
  89.3 3.8 %fusion.75 = (bf16[4096,256]{1,0:T(8,128)(2,1)}, bf16[4096,256]{1,0:T(8,128)(2,1)S(1)}) fusion(bf16[4096,512]{1,0:T(8,128)(2,1)} %all-gather.2.cloned.1.call-done), kind=kLoop, calls=%fused_computation.118 | loop fusion | bytes 8388608 | tf_op jit(solution)/shard_map/split | solution.py:20
  93.1 2.5 broadcast_in_dim.81
  95.6 73.7 %while.15 = (s32[]{:T(128)}, f32[4096,256]{0,1:T(8,128)}, f32[32,128,256]{2,1,0:T(8,128)}, bf16[2,128,5,128]{3,1,2,0:T(8,128)(2,1)}, bf16[2,128,5,128]{3,1,2,0:T...) while((s32[]{:T(128)}, f32[4096,256]{0,1:T(8,128)}, ...), condition=%wide.region_10.11_spmd.clone, body=%wide.region_4.10_spmd.clone.sunk | while | flops 4335778816 | bytes 192303536 | solution.py:145
  95.7 2.8 %gather_fusion = bf16[2,128,256]{2,1,0:T(8,128)(2,1)S(1)} fusion(bf16[32,128,256]{2,1,0:T(8,128)(2,1)} %get-tuple-element.235, s32[1024]{0:T(1024)S(1)} %pad_clamp_fusion.4), kind=kCustom, calls=%fused_computation.clone.clone.1 | custom fusion | bytes 262152 | tf_op jit(solution)/shard_map/while/body/eval_jaxpr/jit(_take)/gather | solution.py:132
  98.9 1.6 bitcast_reduce_fusion.2
  100.7 1.8 fusion.129
  104.5 2.2 fusion.131
  109.8 5.6 %convolution_bitcast_fusion.11 = f32[4096,128]{0,1:T(8,128)S(1)} fusion(bf16[2,128,5,128]{3,1,2,0:T(8,128)(2,1)} %get-tuple-element.236, s32[]{:T(128)S(6)} %copy.70, f32[128,5,4096]{2,0,1:T(8,128)} %copy-done, f32[5,128]{1,0:T(8,128)S(1)} %add.189, f32[5,128]{1,0:T(8,128)S(1)} %max.9), kind=kOutput, calls=%fused_computation.14.clone.1 | convolution fusion | flops 681574400 | bytes 12751876 | tf_op jit(solution)/shard_map/while/body/eval_jaxpr/htk,thd->kd/dot_general | solution.py:44
  116.8 4.4 %fusion.133 = bf16[5,128,4096]{2,1,0:T(8,128)(2,1)S(1)} fusion(f32[5,128]{1,0:T(8,128)S(1)} %fusion.132, bf16[4096,256]{1,0:T(8,128)(2,1)} %copy-done.1, bf16[2,128,5,128]{3,1,2,0:T(8,128)(2,1)} %get-tuple-element.236, s32[]{:T(128)S(6)} %copy.70, f32[5,128]{1,0:T(8,128)S(1)} %add.189, f32[5,128]{1,0:T(8,128)S(1)} %max.9, ...), kind=kOutput, calls=%fused_computation.8.clone.1 | convolution fusion | flops 686817280 | bytes 16948740 | tf_op jit(solution)/shard_map/while/body/eval_jaxpr/thd,kd->htk/dot_general | solution.py:44
  121.2 2.7 %convolution_bitcast_fusion.13 = f32[128,5,128]{2,0,1:T(8,128)S(1)} fusion(bf16[5,128,4096]{2,1,0:T(8,128)(2,1)S(1)} %fusion.133, bf16[4096,256]{1,0:T(8,128)(2,1)} %copy-done.1), kind=kOutput, calls=%fused_computation.36.clone.1 | convolution fusion | flops 671088640 | bytes 6619136 | tf_op jit(solution)/shard_map/while/body/eval_jaxpr/htk,kd->thd/dot_general | solution.py:44
  126.1 2.9 %maximum_add_fusion.2 = f32[4096,256]{0,1:T(8,128)} fusion(f32[4096,128]{0,1:T(8,128)S(1)} %convolution_bitcast_fusion.11, f32[4096,128]{0,1:T(8,128)S(1)} %fusion.134, f32[4096,256]{0,1:T(8,128)} %get-tuple-element.216, pred[]{:T(512)S(6)} %compare.21), kind=kLoop, calls=%fused_computation.17.clone.1 | loop fusion | flops 3145728 | bytes 12582913 | tf_op jit(solution)/shard_map/while/body/eval_jaxpr/add | solution.py:137
  128.9 2.3 scatter_fusion
  131.4 2.8 %gather_fusion = bf16[2,128,256]{2,1,0:T(8,128)(2,1)S(1)} fusion(bf16[32,128,256]{2,1,0:T(8,128)(2,1)} %get-tuple-element.235, s32[1024]{0:T(1024)S(1)} %pad_clamp_fusion.4), kind=kCustom, calls=%fused_computation.clone.clone.1 | custom fusion | bytes 262152 | tf_op jit(solution)/shard_map/while/body/eval_jaxpr/jit(_take)/gather | solution.py:132
  136.3 1.8 fusion.129
  140.2 2.2 fusion.131
  145.5 5.6 %convolution_bitcast_fusion.11 = f32[4096,128]{0,1:T(8,128)S(1)} fusion(bf16[2,128,5,128]{3,1,2,0:T(8,128)(2,1)} %get-tuple-element.236, s32[]{:T(128)S(6)} %copy.70, f32[128,5,4096]{2,0,1:T(8,128)} %copy-done, f32[5,128]{1,0:T(8,128)S(1)} %add.189, f32[5,128]{1,0:T(8,128)S(1)} %max.9), kind=kOutput, calls=%fused_computation.14.clone.1 | convolution fusion | flops 681574400 | bytes 12751876 | tf_op jit(solution)/shard_map/while/body/eval_jaxpr/htk,thd->kd/dot_general | solution.py:44
  152.4 4.4 %fusion.133 = bf16[5,128,4096]{2,1,0:T(8,128)(2,1)S(1)} fusion(f32[5,128]{1,0:T(8,128)S(1)} %fusion.132, bf16[4096,256]{1,0:T(8,128)(2,1)} %copy-done.1, bf16[2,128,5,128]{3,1,2,0:T(8,128)(2,1)} %get-tuple-element.236, s32[]{:T(128)S(6)} %copy.70, f32[5,128]{1,0:T(8,128)S(1)} %add.189, f32[5,128]{1,0:T(8,128)S(1)} %max.9, ...), kind=kOutput, calls=%fused_computation.8.clone.1 | convolution fusion | flops 686817280 | bytes 16948740 | tf_op jit(solution)/shard_map/while/body/eval_jaxpr/thd,kd->htk/dot_general | solution.py:44
  156.8 2.7 %convolution_bitcast_fusion.13 = f32[128,5,128]{2,0,1:T(8,128)S(1)} fusion(bf16[5,128,4096]{2,1,0:T(8,128)(2,1)S(1)} %fusion.133, bf16[4096,256]{1,0:T(8,128)(2,1)} %copy-done.1), kind=kOutput, calls=%fused_computation.36.clone.1 | convolution fusion | flops 671088640 | bytes 6619136 | tf_op jit(solution)/shard_map/while/body/eval_jaxpr/htk,kd->thd/dot_general | solution.py:44
  161.7 5.2 %maximum_add_fusion.2 = f32[4096,256]{0,1:T(8,128)} fusion(f32[4096,128]{0,1:T(8,128)S(1)} %convolution_bitcast_fusion.11, f32[4096,128]{0,1:T(8,128)S(1)} %fusion.134, f32[4096,256]{0,1:T(8,128)} %get-tuple-element.216, pred[]{:T(512)S(6)} %compare.21), kind=kLoop, calls=%fused_computation.17.clone.1 | loop fusion | flops 3145728 | bytes 12582913 | tf_op jit(solution)/shard_map/while/body/eval_jaxpr/add | solution.py:137
  166.9 2.3 scatter_fusion
  169.2 2.5 convert_element_type.49
  171.7 2.8 %reshape_reshape.3 = bf16[4,4,256,256]{2,1,0,3:T(4,128)(2,1)} reshape(bf16[4096,256]{0,1:T(8,128)(2,1)S(1)} %convert_element_type.49) | data formatting | bytes 4194304 | tf_op jit(solution)/shard_map/reshape;reshape | solution.py:25
  174.5 4.3 %copy.37 = bf16[4,4,256,256]{3,2,0,1:T(8,128)(2,1)} copy(bf16[4,4,256,256]{2,1,0,3:T(4,128)(2,1)} %reshape_reshape.3) | data formatting | bytes 4194304 | tf_op jit(solution)/shard_map/reshape;reshape | solution.py:25
  178.8 3.8 %convert_element_type.47 = bf16[32,128,256]{2,1,0:T(8,128)(2,1)} convert(f32[32,128,256]{2,1,0:T(8,128)} %get-tuple-element.60) | non-fusion elementwise | flops 1048576 | bytes 6291456 | tf_op jit(solution)/shard_map/convert_element_type | solution.py:152
  182.7 9.1 %all-to-all-start = ((bf16[16,256,256]{2,1,0:T(8,128)(2,1)}), bf16[16,256,256]{2,1,0:T(8,128)(2,1)S(1)}, u32[]{:S(2)}, u32[]{:S(2)}) async-start(bf16[16,256,256]{2,1,0:T(8,128)(2,1)} %bitcast.13), calls=%async_computation | async-start | bytes 4194304 | tf_op jit(solution)/shard_map/all_to_all | solution.py:151
  191.8 38.0 %reduce-scatter.3.cloned.1.call-done = bf16[4,256,256]{2,1,0:T(8,128)(2,1)} async-done(((bf16[16,256,256]{2,1,0:T(8,128)(2,1)}), bf16[4,256,256]{2,1,0:T(8,128)(2,1)}) %reduce-scatter.3.cloned.1.call-update) | async-done | bytes 524304 | tf_op jit(solution)/shard_map/reduce_scatter | solution.py:28
  231.2 8.4 %all-to-all-done = bf16[16,256,256]{2,1,0:T(8,128)(2,1)S(1)} async-done(((bf16[16,256,256]{2,1,0:T(8,128)(2,1)}), bf16[16,256,256]{2,1,0:T(8,128)(2,1)S(1)}, u32[]{:S(2)}, u32[]{:S(2)}) %all-to-all-start) | async-done | bytes 2097184 | tf_op jit(solution)/shard_map/all_to_all | solution.py:151
  240.6 22.3 %reduce-scatter.5.cloned.1.call-done = bf16[1,256,256]{2,1,0:T(8,128)(2,1)} async-done(((bf16[4,256,256]{2,1,0:T(8,128)(2,1)}), bf16[1,256,256]{2,1,0:T(8,128)(2,1)}) %reduce-scatter.5.cloned.1.call-update) | async-done | bytes 131088 | tf_op jit(solution)/shard_map/reduce_scatter | solution.py:28
  (112 shorter events, 37.6 us)
Async XLA Ops:
  7.2 82.2 %all-gather.2.cloned.1.call-start = ((), (), s32[]{:S(2)}) async-start(), calls=%async_computation.3 | async-start | bytes 4456448 | tf_op jit(solution)/shard_map/all_gather | solution.py:19
  8.9 220.9 %reduce-scatter.3.cloned.1.call-start = ((), (), s32[]{:S(2)}) async-start(), calls=%async_computation.4 | async-start | bytes 2621440 | tf_op jit(solution)/shard_map/reduce_scatter | solution.py:28
  95.6 11.1 %copy-start.1 = (bf16[4096,256]{1,0:T(8,128)(2,1)}, bf16[4096,256]{1,0:T(8,128)(2,1)S(1)}, u32[]{:S(2)}) copy-start(bf16[4096,256]{1,0:T(8,128)(2,1)S(1)} %get-tuple-element.232) | copy-start | bytes 6291460 | tf_op jit(solution)/shard_map/while
  100.5 4.0 %copy-start = (f32[128,5,4096]{2,0,1:T(8,128)}, f32[128,5,4096]{2,0,1:T(8,128)S(1)}, u32[]{:S(2)}) copy-start(f32[128,5,4096]{2,0,1:T(8,128)S(1)} %get-tuple-element.199) | copy-start | bytes 31457284 | tf_op jit(solution)/shard_map/while
  109.6 5.8 %slice-start = ((s8[10485760]{0:T(1024)(128)(4,1)}), s8[2097152]{0:T(1024)(128)(4,1)S(1)}, s32[]{:S(2)}) async-start(s8[10485760]{0:T(1024)(128)(4,1)} %bitcast.270), calls=%async_computation.6 | async-start | bytes 4194304 | tf_op jit(solution)/shard_map/while
  109.8 5.8 %slice-start.1 = ((s8[10485760]{0:T(1024)(128)(4,1)}), s8[4194304]{0:T(1024)(128)(4,1)S(1)}, s32[]{:S(2)}) async-start(s8[10485760]{0:T(1024)(128)(4,1)} %bitcast.270), calls=%async_computation.7 | async-start | bytes 8388608 | tf_op jit(solution)/shard_map/while
  109.8 7.0 %slice-start.2 = ((s8[10485760]{0:T(1024)(128)(4,1)}), s8[4194304]{0:T(1024)(128)(4,1)S(1)}, s32[]{:S(2)}) async-start(s8[10485760]{0:T(1024)(128)(4,1)} %bitcast.270), calls=%async_computation.8 | async-start | bytes 8388608 | tf_op jit(solution)/shard_map/while
  123.9 1.1 copy-start.3
  125.3 0.7 copy-start.4
  126.1 5.2 %copy-start.2 = (bf16[4096,256]{1,0:T(8,128)(2,1)S(1)}, bf16[4096,256]{1,0:T(8,128)(2,1)}, u32[]{:S(2)}) copy-start(bf16[4096,256]{1,0:T(8,128)(2,1)} %copy-done.1) | copy-start | bytes 6291460 | tf_op jit(solution)/shard_map/while
  131.3 11.1 %copy-start.1 = (bf16[4096,256]{1,0:T(8,128)(2,1)}, bf16[4096,256]{1,0:T(8,128)(2,1)S(1)}, u32[]{:S(2)}) copy-start(bf16[4096,256]{1,0:T(8,128)(2,1)S(1)} %get-tuple-element.232) | copy-start | bytes 6291460 | tf_op jit(solution)/shard_map/while
  136.2 4.0 %copy-start = (f32[128,5,4096]{2,0,1:T(8,128)}, f32[128,5,4096]{2,0,1:T(8,128)S(1)}, u32[]{:S(2)}) copy-start(f32[128,5,4096]{2,0,1:T(8,128)S(1)} %get-tuple-element.199) | copy-start | bytes 31457284 | tf_op jit(solution)/shard_map/while
  145.3 5.8 %slice-start = ((s8[10485760]{0:T(1024)(128)(4,1)}), s8[2097152]{0:T(1024)(128)(4,1)S(1)}, s32[]{:S(2)}) async-start(s8[10485760]{0:T(1024)(128)(4,1)} %bitcast.270), calls=%async_computation.6 | async-start | bytes 4194304 | tf_op jit(solution)/shard_map/while
  145.4 5.8 %slice-start.1 = ((s8[10485760]{0:T(1024)(128)(4,1)}), s8[4194304]{0:T(1024)(128)(4,1)S(1)}, s32[]{:S(2)}) async-start(s8[10485760]{0:T(1024)(128)(4,1)} %bitcast.270), calls=%async_computation.7 | async-start | bytes 8388608 | tf_op jit(solution)/shard_map/while
  145.5 7.0 %slice-start.2 = ((s8[10485760]{0:T(1024)(128)(4,1)}), s8[4194304]{0:T(1024)(128)(4,1)S(1)}, s32[]{:S(2)}) async-start(s8[10485760]{0:T(1024)(128)(4,1)} %bitcast.270), calls=%async_computation.8 | async-start | bytes 8388608 | tf_op jit(solution)/shard_map/while
  159.6 1.1 copy-start.3
  161.0 0.7 copy-start.4
  161.7 7.5 %copy-start.2 = (bf16[4096,256]{1,0:T(8,128)(2,1)S(1)}, bf16[4096,256]{1,0:T(8,128)(2,1)}, u32[]{:S(2)}) copy-start(bf16[4096,256]{1,0:T(8,128)(2,1)} %copy-done.1) | copy-start | bytes 6291460 | tf_op jit(solution)/shard_map/while
  178.8 51.0 %copy-start.5 = (bf16[2,128,5,128]{3,1,2,0:T(8,128)(2,1)S(1)}, bf16[2,128,5,128]{3,1,2,0:T(8,128)(2,1)}, u32[]{:S(2)}) copy-start(bf16[2,128,5,128]{3,1,2,0:T(8,128)(2,1)} %get-tuple-element.59) | copy-start | bytes 983044
  182.7 57.0 %all-to-all-start = ((bf16[16,256,256]{2,1,0:T(8,128)(2,1)}), bf16[16,256,256]{2,1,0:T(8,128)(2,1)S(1)}, u32[]{:S(2)}, u32[]{:S(2)}) async-start(bf16[16,256,256]{2,1,0:T(8,128)(2,1)} %bitcast.13), calls=%async_computation | async-start | bytes 4194304 | tf_op jit(solution)/shard_map/all_to_all | solution.py:151
  191.8 71.1 %reduce-scatter.5.cloned.1.call-start = ((), (), s32[]{:S(2)}) async-start(), calls=%async_computation.5 | async-start | bytes 655360 | tf_op jit(solution)/shard_map/reduce_scatter | solution.py:28
Sparse Core Ops, SparseCore 0:
  10.4 78.8 all-gather.1
  179.0 50.8 reduce-scatter.2
  232.9 29.9 reduce-scatter.4
